TPU v7x, 32 devices: a whole 2x2x4 slice. The times are simulated.
32 devices in a mesh: fsdp: 4 (over y, core), sp: 8 (over z, x).
Axes of the slice: x: 2, y: 2, z: 4, core: 2. Of those that a mesh axis runs over, the one named last changes fastest.
Arguments:
- hidden: bfloat16 [2048, 8192], P('sp', 'fsdp'), may hold values from -23 to 23
- w_query: bfloat16 [8192, 1024], P('fsdp', 'sp'), may hold values from -0.125 to 0.125
- w_keyvalue: bfloat16 [8192, 256], P('fsdp', 'sp'), may hold values from -0.125 to 0.125
- w_output: bfloat16 [1024, 8192], P('sp', 'fsdp'), may hold values from -0.75 to 0.75
- segment_ids: int32 [2048], P('sp'), may hold values from 0 to 7, never falling along the last dimension, each value on 1 to 512 neighbouring positions
Outputs:
- attended: bfloat16 [2048, 8192], P('sp', 'fsdp')
Inputs may be any that keep to these rules, and one draw needn't show every extreme that they name: `segment_ids`: segment ids never fall along the sequence; every episode has between 1 and 512 tokens.
All inputs are finite; a program needn't handle non-finite values.
Results may differ from a plain program's by a relative error of at most 0.0085.
The roundings to bfloat16 on the way count: a program that leaves them out, or rounds other values in their place, can miss the bound.
Values may be sent and summed in bfloat16 or wider, within the bound.
A program may use at most 128 MiB of HBM per device.

v0:
```python
import math

import jax
import jax.numpy as jnp
from jax import lax
from jax.sharding import PartitionSpec as P

HD = 128
GROUP = 8


ROPE_BASE = 500000.0
NEG_FILL = -1e30


def rotate(values, positions, head_count, width):
    row_count = values.shape[0]
    shaped = values.reshape(row_count, head_count, width)
    half_width = width // 2
    frequency = jnp.exp(
        jnp.arange(half_width, dtype=jnp.float32) * (-2.0 * math.log(ROPE_BASE) / width)
    )
    angles = positions.astype(jnp.float32)[:, None] * frequency[None, :]
    cosine = jnp.cos(angles)[:, None, :]
    sine_part = jnp.sin(angles)[:, None, :]
    lower_half = shaped[:, :, :half_width]
    upper_half = shaped[:, :, half_width:]
    turned = jnp.concatenate(
        [
            lower_half * cosine - upper_half * sine_part,
            upper_half * cosine + lower_half * sine_part,
        ],
        axis=2,
    )
    return turned.reshape(row_count, head_count * width)


def split_keys(kv_sum, positions, kv_count, width):
    row_count = kv_sum.shape[0]
    shaped = kv_sum.reshape(row_count, kv_count, 2, width)
    key_part = rotate(
        shaped[:, :, 0, :].reshape(row_count, kv_count * width), positions, kv_count, width
    )
    key_part = key_part.reshape(row_count, kv_count, 1, width)
    return jnp.concatenate([key_part, shaped[:, :, 1:2, :]], axis=2).astype(jnp.bfloat16)


def merge_keys(
    state_in, query_tile, query_pos_tile, query_seg_tile, key_tile, key_pos_tile, key_seg_tile
):
    running_max, running_sum, weighted = state_in
    allowed = (key_pos_tile[None, :] <= query_pos_tile[:, None]) & (
        key_seg_tile[None, :] == query_seg_tile[:, None]
    )
    key_part = key_tile[:, :HD]
    value_part = key_tile[:, HD:]
    scores = lax.dot_general(
        query_tile, key_part, (((1,), (1,)), ((), ())), preferred_element_type=jnp.float32
    ) * HD ** (-0.5)
    masked = jnp.where(allowed, scores, NEG_FILL)
    new_max = jnp.maximum(running_max, jnp.max(masked, axis=1))
    weights = jnp.where(allowed, jnp.exp(masked - new_max[:, None]), 0.0)
    new_sum = jnp.sum(weights, axis=1)
    new_weighted = jnp.dot(
        weights.astype(jnp.bfloat16), value_part, preferred_element_type=jnp.float32
    )
    return (new_max, new_sum, new_weighted)


def on_device(hidden, w_query, w_keyvalue, w_output, segment_ids):
    fsdp_count = lax.axis_size("fsdp")
    seq_count = lax.axis_size("sp")
    fsdp_index = lax.axis_index("fsdp")
    seq_index = lax.axis_index("sp")
    tok_rows = hidden.shape[0]
    sub_rows = tok_rows // fsdp_count
    kv_count = seq_count // GROUP
    query_rows = seq_count * sub_rows
    offsets = jnp.arange(query_rows, dtype=jnp.int32)
    query_pos = offsets // sub_rows * tok_rows + fsdp_index * sub_rows + offsets % sub_rows
    own_positions = (
        seq_index * tok_rows + fsdp_index * sub_rows + jnp.arange(sub_rows, dtype=jnp.int32)
    )

    def project(weight_block):
        return jnp.dot(hidden, weight_block, preferred_element_type=jnp.float32)

    query_part = project(lax.all_gather(w_query, "sp", axis=1, tiled=True))
    kv_part = project(lax.all_gather(w_keyvalue, "sp", axis=1, tiled=True))
    query_sum, kv_sum = (
        lax.psum_scatter(query_part, "fsdp", scatter_dimension=0, tiled=True),
        lax.psum_scatter(kv_part, "fsdp", scatter_dimension=0, tiled=True),
    )
    query_local = rotate(query_sum, own_positions, seq_count, HD).astype(jnp.bfloat16)
    pairs = split_keys(kv_sum, own_positions, kv_count, HD)
    expanded = jnp.repeat(pairs, GROUP, axis=1).reshape(sub_rows, seq_count * 2 * HD)
    query_head, kv_head = (
        lax.all_to_all(query_local, "sp", split_axis=1, concat_axis=0, tiled=True),
        lax.all_to_all(expanded, "sp", split_axis=1, concat_axis=0, tiled=True),
    )
    segment_all = lax.all_gather(segment_ids, "sp", axis=0, tiled=True)
    query_seg = segment_all[query_pos]
    initial = (
        jnp.full((query_rows,), NEG_FILL, jnp.float32),
        jnp.zeros((query_rows,), jnp.float32),
        jnp.zeros((query_rows, HD), jnp.float32),
    )
    block_keys = lax.all_gather(kv_head, "fsdp", axis=0, tiled=True)
    piece_rows = block_keys.shape[0]
    row_ids = jnp.arange(piece_rows, dtype=jnp.int32)
    source_id = row_ids // query_rows
    within = row_ids % query_rows
    key_pos = within // sub_rows * tok_rows + source_id * sub_rows + within % sub_rows
    key_seg = segment_all[key_pos]
    final_max, final_sum, final_weighted = merge_keys(
        initial, query_head, query_pos, query_seg, block_keys, key_pos, key_seg
    )
    attention = (final_weighted / final_sum[:, None]).astype(jnp.bfloat16)
    back_rows = lax.all_to_all(attention, "sp", split_axis=0, concat_axis=1, tiled=True)
    mixed_rows = lax.all_gather(back_rows, "fsdp", axis=0, tiled=True)
    result = jnp.dot(
        mixed_rows,
        lax.all_gather(w_output, "sp", axis=0, tiled=True),
        preferred_element_type=jnp.float32,
    )
    return result.astype(jnp.bfloat16)


def solution(mesh):
    in_specs = (P("sp", "fsdp"), P("fsdp", "sp"), P("fsdp", "sp"), P("sp", "fsdp"), P("sp"))
    out_specs = P("sp", "fsdp")
    return jax.shard_map(
        on_device, mesh=mesh, in_specs=in_specs, out_specs=out_specs, check_vma=False
    )
```

profile of v0, /device:TPU:24, one launch (start us, length us, event | category | flops | bytes accessed | tf_op | source)
XLA Modules:
  0.0 277.4 jit_solution(3011996384781910842)
XLA Ops:
  6.5 0.7 all-gather.8.cloned.1.call-update
  7.3 0.7 all-gather.6.cloned.1.call-update
  8.1 41.4 %all-gather.8.cloned.1.call-done = bf16[2048,256]{0,1:T(8,128)(2,1)} async-done(((bf16[2048,32]{0,1:T(8,128)(2,1)}), bf16[2048,256]{0,1:T(8,128)(2,1)}) %all-gather.8.cloned.1.call-update) | async-done | bytes 1048592 | tf_op jit(solution)/shard_map/all_gather | solution.py:89
  49.5 2.4 fusion.62
  52.0 72.3 %all-gather.6.cloned.1.call-done = bf16[2048,1024]{1,0:T(8,128)(2,1)} async-done(((bf16[2048,128]{1,0:T(8,128)(2,1)}), bf16[2048,1024]{1,0:T(8,128)(2,1)}) %all-gather.6.cloned.1.call-update) | async-done | bytes 4194320 | tf_op jit(solution)/shard_map/all_gather | solution.py:88
  124.3 4.4 %fusion.61 = f32[256,1024]{1,0:T(8,128)} fusion(bf16[256,2048]{1,0:T(8,128)(2,1)S(1)} %copy-done, bf16[2048,1024]{1,0:T(8,128)(2,1)} %all-gather.6.cloned.1.call-done), kind=kOutput, calls=%fused_computation.109 | convolution fusion | flops 1073741824 | bytes 6291456 | tf_op jit(solution)/shard_map/dot_general | solution.py:86
  128.8 18.1 %reduce-scatter.5.cloned.1.call-done = f32[64,256]{1,0:T(8,128)} async-done(((f32[256,256]{1,0:T(8,128)}), f32[64,256]{1,0:T(8,128)}) %reduce-scatter.5.cloned.1.call-update) | async-done | bytes 65552 | tf_op jit(solution)/shard_map/reduce_scatter | solution.py:92
  146.9 0.9 reshape.398
  148.2 11.9 %all_to_all.51 = bf16[64,8,256]{2,0,1:T(8,128)(2,1)} all-to-all(bf16[64,8,256]{2,0,1:T(8,128)(2,1)S(1)} %broadcast_in_dim.10), channel_id=1, replica_groups=mesh['fsdp'=4,'sp'=8] {'sp'}, dimensions={1} | all-to-all | bytes 524288 | tf_op jit(solution)/shard_map/all_to_all | solution.py:99
  160.2 0.5 all-gather.12.cloned.1.call-update
  161.0 13.2 %reduce-scatter.3.cloned.1.call-done = f32[64,1024]{1,0:T(8,128)} async-done(((f32[256,1024]{1,0:T(8,128)}), f32[64,1024]{1,0:T(8,128)}) %reduce-scatter.3.cloned.1.call-update) | async-done | bytes 262160 | tf_op jit(solution)/shard_map/reduce_scatter | solution.py:91
  174.2 1.0 copy.25
  175.4 0.8 pad_maximum_fusion
  176.2 6.0 %all-to-all-start = ((bf16[64,8,128]{2,0,1:T(8,128)(2,1)}), bf16[64,8,128]{2,0,1:T(8,128)(2,1)S(1)}, u32[]{:S(2)}, u32[]{:S(2)}) async-start(bf16[64,8,128]{2,0,1:T(8,128)(2,1)} %pad_maximum_fusion), calls=%async_computation.1 | async-start | bytes 262144 | tf_op jit(solution)/shard_map/all_to_all | solution.py:98
  182.2 15.9 %all-gather = s32[8,1,256]{2,1,0:T(1,128)S(1)} all-gather(s32[1,1,256]{2,1,0:T(1,128)S(1)} %bitcast.48), channel_id=1, replica_groups=mesh['fsdp'=4,'sp'=8] {'sp'}, dimensions={0}, use_global_device_ids=true | all-gather | bytes 9216 | tf_op jit(solution)/shard_map/all_gather | solution.py:101
  198.2 3.1 %gather_fusion.1 = s32[512]{0:T(512)S(1)} fusion(s32[2048]{0:T(1024)S(1)} %bitcast.37, s32[1024]{0:T(1024)S(1)} %pad_clamp_fusion), kind=kCustom, calls=%fused_computation.1 | custom fusion | bytes 6144 | tf_op jit(solution)/shard_map/gather | solution.py:102
  201.3 11.8 %gather_fusion = s32[2048]{0:T(1024)S(1)} fusion(s32[2048]{0:T(1024)S(1)} %bitcast.38, s32[2048]{0:T(1024)S(1)} %broadcast_clamp_fusion), kind=kCustom, calls=%fused_computation | custom fusion | bytes 24576 | tf_op jit(solution)/shard_map/gather | solution.py:114
  213.2 2.4 fusion
  215.5 1.7 fusion.1
  217.2 1.3 fusion.8
  218.5 13.2 %all_to_all.52 = bf16[8,64,128]{2,1,0:T(8,128)(2,1)S(1)} all-to-all(bf16[8,64,128]{2,1,0:T(8,128)(2,1)S(1)} %bitcast.44), channel_id=1, replica_groups=mesh['fsdp'=4,'sp'=8] {'sp'}, dimensions={0} | all-to-all | bytes 262144 | tf_op jit(solution)/shard_map/all_to_all | solution.py:119
  231.7 6.5 %all_gather.22 = bf16[256,1024]{1,0:T(8,128)(2,1)S(1)} all-gather(bf16[64,1024]{1,0:T(8,128)(2,1)S(1)} %copy_bitcast_fusion), channel_id=1, replica_groups=mesh['fsdp'=4,'sp'=8] {'fsdp'}, dimensions={0}, use_global_device_ids=true | all-gather | bytes 655360 | tf_op jit(solution)/shard_map/all_gather | solution.py:120
  238.2 27.9 %all-gather.12.cloned.1.call-done = bf16[1024,2048]{1,0:T(8,128)(2,1)} async-done(((bf16[128,2048]{1,0:T(8,128)(2,1)}), bf16[1024,2048]{1,0:T(8,128)(2,1)}) %all-gather.12.cloned.1.call-update) | async-done | bytes 4194320 | tf_op jit(solution)/shard_map/all_gather | solution.py:123
  266.1 4.4 %convolution_convert_fusion = bf16[256,2048]{1,0:T(8,128)(2,1)} fusion(bf16[256,1024]{1,0:T(8,128)(2,1)S(1)} %all_gather.22, bf16[1024,2048]{1,0:T(8,128)(2,1)} %all-gather.12.cloned.1.call-done), kind=kOutput, calls=%fused_computation.6 | convolution fusion | flops 1074266112 | bytes 5767168 | tf_op jit(solution)/shard_map/dot_general | solution.py:121
  (37 shorter events, 1.2 us)
Async XLA Ops:
  6.5 42.9 %copy-start = (bf16[256,2048]{1,0:T(8,128)(2,1)S(1)}, bf16[256,2048]{1,0:T(8,128)(2,1)}, u32[]{:S(2)}) copy-start(bf16[256,2048]{1,0:T(8,128)(2,1)} %param.5) | copy-start | bytes 3145732
  6.5 42.9 %all-gather.8.cloned.1.call-start = ((), (), s32[]{:S(2)}) async-start(), calls=%async_computation.7 | async-start | bytes 1179648 | tf_op jit(solution)/shard_map/all_gather | solution.py:89
  7.3 117.0 %all-gather.6.cloned.1.call-start = ((), (), s32[]{:S(2)}) async-start(), calls=%async_computation.5 | async-start | bytes 4718592 | tf_op jit(solution)/shard_map/all_gather | solution.py:88
  8.0 138.9 %reduce-scatter.5.cloned.1.call-start = ((), (), s32[]{:S(2)}) async-start(), calls=%async_computation.8 | async-start | bytes 327680 | tf_op jit(solution)/shard_map/reduce_scatter | solution.py:92
  51.9 122.2 %reduce-scatter.3.cloned.1.call-start = ((), (), s32[]{:S(2)}) async-start(), calls=%async_computation.6 | async-start | bytes 1310720 | tf_op jit(solution)/shard_map/reduce_scatter | solution.py:91
  128.7 53.5 %copy-start.1 = (s32[256]{0:T(256)S(1)}, s32[256]{0:T(256)}, u32[]{:S(2)}) copy-start(s32[256]{0:T(256)} %param.9) | copy-start | bytes 3076
  128.7 84.4 %all-gather.10.cloned.1.call-start = ((), (), s32[]{:S(2)}) async-start(), calls=%async_computation.9 | async-start | bytes 1310720 | tf_op jit(solution)/shard_map/all_gather | solution.py:108
  160.1 106.0 %all-gather.12.cloned.1.call-start = ((), (), s32[]{:S(2)}) async-start(), calls=%async_computation.10 | async-start | bytes 4718592 | tf_op jit(solution)/shard_map/all_gather | solution.py:123
  176.2 37.0 %all-to-all-start = ((bf16[64,8,128]{2,0,1:T(8,128)(2,1)}), bf16[64,8,128]{2,0,1:T(8,128)(2,1)S(1)}, u32[]{:S(2)}, u32[]{:S(2)}) async-start(bf16[64,8,128]{2,0,1:T(8,128)(2,1)} %pad_maximum_fusion), calls=%async_computation.1 | async-start | bytes 262144 | tf_op jit(solution)/shard_map/all_to_all | solution.py:98
  213.2 4.1 %copy-start.2 = (bf16[2048,256]{1,0:T(8,128)(2,1)S(1)}, bf16[2048,256]{1,0:T(8,128)(2,1)}, u32[]{:S(2)}) copy-start(bf16[2048,256]{1,0:T(8,128)(2,1)} %all-gather.10.cloned.1.call-done) | copy-start | bytes 3145732
Sparse Core Ops, SparseCore 0:
  9.5 39.9 all-gather.7
  51.5 72.7 all-gather.5
  126.7 20.1 reduce-scatter.4
  149.3 24.8 reduce-scatter.2
  175.6 16.6 all-gather.9
  194.3 71.7 all-gather.11
where the time goes:
time: 281 us; the launch traced here: 277 us
  waiting for transfers between devices  175 us (62%)
  blocking collectives  47.5 us (17%)
  local copies, waits for them, and re-layouts  17 us (6%)
  matrix products  14.9 us (5%)
  between operations  13.7 us (5%)
  starting transfers between devices  6.22 us (2%)
  other arithmetic  3.13 us (1%)
    all_gather x1, waiting for transfers between devices, on_device(): query_part = project(lax.all_gather(w_query, 'sp', axis=1, tiled=True))  72.3 us
    all_gather x1, waiting for transfers between devices, on_device(): kv_part = project(lax.all_gather(w_keyvalue, 'sp', axis=1, tiled=True))  41.4 us
    all_gather x1, waiting for transfers between devices, on_device(): lax.all_gather(w_output, 'sp', axis=0, tiled=True)  27.9 us
    reduce_scatter x1, waiting for transfers between devices, on_device(): lax.psum_scatter(kv_part, 'fsdp', scatter_dimension=0, tiled=True)  18.1 us
    all_gather x1, blocking collectives, on_device(): segment_all = lax.all_gather(segment_ids, 'sp', axis=0, tiled=True)  15.9 us
    all_to_all x1, blocking collectives, on_device(): lax.all_to_all(attention, 'sp', split_axis=0, concat_axis=1, tiled=True)  13.2 us
    reduce_scatter x1, waiting for transfers between devices, on_device(): lax.psum_scatter(query_part, 'fsdp', scatter_dimension=0, tiled=True)  13.2 us
    all_to_all x1, blocking collectives, on_device(): lax.all_to_all(expanded, 'sp', split_axis=1, concat_axis=0, tiled=True)  11.9 us
  transfers between devices with their start and end apart: 7, of which 5 were waited for; matrix products, arithmetic and copies ran while one was open for 11% of the time, Pallas kernels for 0%

commit v1 on v0

--- a/solution.py
+++ b/solution.py
@@ -1,8 +1,11 @@
+import functools
 import math
 
 import jax
 import jax.numpy as jnp
 from jax import lax
+from jax.experimental import pallas as pl
+from jax.experimental.pallas import tpu as pltpu
 from jax.sharding import PartitionSpec as P
 
 HD = 128
@@ -126,9 +129,487 @@
     return result.astype(jnp.bfloat16)
 
 
+NEG_POS = -1
+WO_CHUNKS = 2
+
+
+def fused_kernel(
+    nf, nz, nx, hid, wq, wkv, wo, seg, out,
+    h_buf, wq_buf, wkv_buf, wo_buf, seg_buf,
+    q_part, q_recv, kv_part, kv_recv, kv_piece, kv_all, mix_own, mix_buf,
+    s_loc, s_hid, r_hid, s_seg, r_seg, s_wkv, r_wkv, s_wqr, s_wql, r_wq,
+    s_q, r_q, s_kvp, r_kvp, s_kv, r_kv, s_wor, s_wol, s_wox, r_wo, s_mix, r_mix,
+):
+    f = lax.axis_index("fsdp")
+    s = lax.axis_index("sp")
+    z, x = s // nx, s % nx
+    tok, kdim = hid.shape
+    rows = tok * nx
+    sub = rows // nf
+    kvw = wkv.shape[0]
+    other = 1 - x
+    chunk = wo.shape[1] // WO_CHUNKS
+    f32, bf16 = jnp.float32, jnp.bfloat16
+
+    def dev(ff, zz, xx):
+        return (ff, zz * nx + xx)
+
+    def remote(src, dst, ss, rs, target):
+        return pltpu.make_async_remote_copy(
+            src_ref=src, dst_ref=dst, send_sem=ss, recv_sem=rs,
+            device_id=target, device_id_type=pl.DeviceIdType.MESH,
+        )
+
+    def tile(ref, count):
+        return pl.ds(pl.multiple_of(ref * count, count), count)
+
+    here = (f, s)
+    own_h = pltpu.make_async_copy(hid, h_buf.at[tile(x, tok)], s_loc.at[0])
+    own_wq = pltpu.make_async_copy(wq, wq_buf.at[z], s_loc.at[1])
+    own_wkv = pltpu.make_async_copy(wkv, wkv_buf.at[tile(z, kvw)], s_loc.at[2])
+    own_wo = pltpu.make_async_copy(wo, wo_buf.at[tile(s, HD)], s_loc.at[3])
+    own_seg = pltpu.make_async_copy(seg, seg_buf.at[1, x], s_loc.at[4])
+    hid_send = remote(hid, h_buf.at[tile(x, tok)], s_hid, r_hid, dev(f, z, other))
+
+    def hid_wait():
+        remote(hid, h_buf.at[tile(other, tok)], s_hid, r_hid, here).wait_recv()
+
+    def wkv_send(d):
+        zz = lax.rem(z + d, nz)
+        return remote(
+            wkv, wkv_buf.at[tile(z, kvw)], s_wkv.at[d - 1], r_wkv.at[z], dev(f, zz, x)
+        )
+
+    def wkv_wait(d):
+        zz = lax.rem(z + d, nz)
+        remote(
+            wkv, wkv_buf.at[tile(zz, kvw)], s_wkv.at[d - 1], r_wkv.at[zz], here
+        ).wait_recv()
+
+    def wq_copy(src, j, to_right):
+        sems = s_wqr if to_right else s_wql
+        return remote(
+            src, wq_buf.at[j], sems.at[j], r_wq.at[j],
+            dev(f, z + 1 if to_right else z - 1, x),
+        )
+
+    def wo_slice(zz, xx, c):
+        return wo_buf.at[tile(zz * nx + xx, HD), c * chunk : (c + 1) * chunk]
+
+    def wo_src(j, c, own):
+        return wo.at[:, c * chunk : (c + 1) * chunk] if own else wo_slice(j, x, c)
+
+    def wo_copy(j, c, to_right, own=False):
+        sems = s_wor if to_right else s_wol
+        return remote(
+            wo_src(j, c, own), wo_slice(j, x, c), sems.at[j, c], r_wo.at[j * nx + x, c],
+            dev(f, z + 1 if to_right else z - 1, x),
+        )
+
+    def wo_cross(j, c, own=False):
+        return remote(
+            wo_src(j, c, own), wo_slice(j, x, c), s_wox.at[j, c], r_wo.at[j * nx + x, c],
+            dev(f, z, other),
+        )
+
+    def wo_wait(j, xx, c):
+        remote(
+            wo_slice(j, xx, c), wo_slice(j, xx, c), s_wox.at[j, c], r_wo.at[j * nx + xx, c], here
+        ).wait_recv()
+
+    def wo_own(to_right):
+        for c in range(WO_CHUNKS):
+            wo_copy(z, c, to_right, own=True).start()
+
+    seg_same = remote(seg, seg_buf.at[1, x], s_seg.at[0], r_seg.at[1, x], dev(f, z, other))
+
+    def seg_next(xx):
+        return remote(
+            seg, seg_buf.at[0, x], s_seg.at[1 + xx], r_seg.at[0, x], dev(f, z + 1, xx)
+        )
+
+    for d in range(1, nz):
+        wkv_send(d).start()
+
+    @pl.when(z < nz - 1)
+    def _():
+        wq_copy(wq, z, True).start()
+
+    @pl.when(z > 0)
+    def _():
+        wq_copy(wq, z, False).start()
+
+    hid_send.start()
+    seg_same.start()
+
+    @pl.when(z < nz - 1)
+    def _():
+        for xx in range(nx):
+            seg_next(xx).start()
+
+    for copy in (own_h, own_wq, own_wkv, own_wo, own_seg):
+        copy.start()
+
+    @pl.when(z == 0)
+    def _():
+        wo_own(True)
+        kv_all[0] = jnp.zeros(kv_all.shape[1:], bf16)
+        seg_buf[0] = jnp.full(seg_buf.shape[1:], NEG_POS, jnp.int32)
+
+    @pl.when(z == nz - 1)
+    def _():
+        wo_own(False)
+
+    def table(row_count, first, lane_index):
+        position = (first + lax.broadcasted_iota(jnp.int32, (row_count, HD), 0)).astype(f32)
+        frequency = jnp.exp(lane_index.astype(f32) * (-2.0 * math.log(ROPE_BASE) / HD))
+        return position * frequency
+
+    lane = lax.broadcasted_iota(jnp.int32, (1, HD), 1)
+    half = HD // 2
+    quarter = half // nx
+    kv_angle = table(sub, z * rows + f * sub, x * quarter + lane % quarter)
+    is_key = lane < half
+    kv_cos = jnp.where(is_key, jnp.cos(kv_angle), 1.0)
+    kv_sin = jnp.where(is_key, jnp.sin(kv_angle), 0.0)
+    kv_sin = jnp.where(lane < quarter, -kv_sin, kv_sin)
+
+    def wq_step(d):
+        @pl.when(z >= d)
+        def _():
+            j = z - d
+            wq_copy(wq_buf.at[j], j, True).wait_recv()
+
+            @pl.when(z < nz - 1)
+            def _():
+                wq_copy(wq_buf.at[j], j, True).start()
+
+                @pl.when(z == d)
+                def _():
+                    wo_own(True)
+
+        @pl.when(z + d < nz)
+        def _():
+            j = z + d
+            wq_copy(wq_buf.at[j], j, False).wait_recv()
+
+            @pl.when(z > 0)
+            def _():
+                wq_copy(wq_buf.at[j], j, False).start()
+
+                @pl.when(z + d == nz - 1)
+                def _():
+                    wo_own(False)
+
+    def q_send(j):
+        return remote(q_part.at[j], q_recv.at[f], s_q.at[j], r_q.at[f], (j, s))
+
+    def q_project(j):
+        q_part[j] = jnp.dot(h_buf[...], wq_buf[j], preferred_element_type=f32)
+
+        @pl.when(j != f)
+        def _():
+            q_send(j).start()
+
+    def q_step(d):
+        @pl.when(z >= d)
+        def _():
+            q_project(z - d)
+
+        @pl.when(z + d < nz)
+        def _():
+            q_project(z + d)
+
+    wq_step(1)
+    own_h.wait()
+    own_wq.wait()
+    own_wkv.wait()
+    hid_wait()
+    for c in range(WO_CHUNKS):
+        wo_cross(z, c, own=True).start()
+    for d in range(1, nz):
+        wkv_wait(d)
+    kv_part[...] = lax.dot_general(
+        h_buf[...], wkv_buf[...], (((1,), (1,)), ((), ())), preferred_element_type=f32
+    )
+
+    def kvp_send(d):
+        ff = lax.rem(f + d, nf)
+        return remote(
+            kv_part.at[tile(ff, sub)], kv_recv.at[f], s_kvp.at[d - 1], r_kvp.at[f], (ff, s)
+        )
+
+    def kvp_wait(d):
+        ff = lax.rem(f + d, nf)
+        remote(
+            kv_part.at[tile(ff, sub)], kv_recv.at[ff], s_kvp.at[d - 1], r_kvp.at[ff], here
+        ).wait_recv()
+
+    for d in range(1, nf):
+        kvp_send(d).start()
+    q_project(z)
+    q_step(1)
+    total = kv_part[tile(f, sub), :]
+    for d in range(1, nf):
+        kvp_wait(d)
+        total = total + kv_recv[lax.rem(f + d, nf)]
+    partner = jnp.where(
+        lane < quarter, pltpu.roll(total, HD - quarter, 1), pltpu.roll(total, quarter, 1)
+    )
+    kv_piece[...] = (total * kv_cos + partner * kv_sin).astype(bf16)
+    piece_rows = tile(f, sub)
+    own_piece = pltpu.make_async_copy(kv_piece, kv_all.at[1, x, piece_rows], s_loc.at[5])
+    own_piece.start()
+
+    def kv_send(plane, dx, d):
+        ff, xx = lax.rem(f + d, nf), lax.rem(x + dx, nx)
+        return remote(
+            kv_piece, kv_all.at[plane, x, piece_rows],
+            s_kv.at[plane, dx, d], r_kv.at[plane, x, f], dev(ff, z + 1 - plane, xx),
+        )
+
+    def kv_wait(plane, dx, d):
+        ff, xx = lax.rem(f + d, nf), lax.rem(x + dx, nx)
+        remote(
+            kv_piece, kv_all.at[plane, xx, tile(ff, sub)],
+            s_kv.at[plane, dx, d], r_kv.at[plane, xx, ff], here,
+        ).wait_recv()
+
+    pairs = [(dx, d) for dx in range(nx) for d in range(nf)]
+    for pair in pairs[1:]:
+        kv_send(1, *pair).start()
+
+    @pl.when(z < nz - 1)
+    def _():
+        for pair in pairs:
+            kv_send(0, *pair).start()
+
+    for d in range(2, nz):
+        wq_step(d)
+        q_step(d)
+
+    def wo_side(j, to_right):
+        for c in range(WO_CHUNKS):
+            wo_wait(j, x, c)
+            if to_right is not None:
+                wo_copy(j, c, to_right).start()
+            wo_cross(j, c).start()
+
+    def wo_mid(d):
+        @pl.when((z >= d) & (z < nz - 1))
+        def _():
+            wo_side(z - d, True)
+
+        @pl.when((z + d < nz) & (z > 0))
+        def _():
+            wo_side(z + d, False)
+
+    def wo_end(d):
+        if d < nz:
+            @pl.when((z >= d) & (z == nz - 1))
+            def _():
+                wo_side(z - d, None)
+
+            @pl.when((z + d < nz) & (z == 0))
+            def _():
+                wo_side(z + d, None)
+
+    for d in range(1, nz - 1):
+        wo_mid(d)
+
+    q_angle = table(rows, z * rows, lane % half)
+    q_cos = jnp.cos(q_angle)
+    q_sin = jnp.where(lane < half, -jnp.sin(q_angle), jnp.sin(q_angle))
+    q_total = q_part[f]
+    for d in range(1, nf):
+        ff = lax.rem(f + d, nf)
+        remote(q_part.at[0], q_recv.at[ff], s_q.at[0], r_q.at[ff], here).wait_recv()
+        q_total = q_total + q_recv[ff]
+    q_turned = q_total * q_cos + pltpu.roll(q_total, half, 1) * q_sin
+    q_head = q_turned.astype(bf16).astype(f32)
+    quarters = []
+    for xx in range(nx):
+        low = q_head if xx == 0 else pltpu.roll(q_head, HD - xx * quarter, 1)
+        high = pltpu.roll(q_head, (HD - half - xx * quarter + quarter) % HD, 1)
+        picked = jnp.where(lane < quarter, low, jnp.where(lane < half, high, 0.0))
+        quarters.append(picked.astype(bf16))
+
+    own_seg.wait()
+    seg_wait = lambda plane, xx: remote(
+        seg, seg_buf.at[plane, xx], s_seg.at[0], r_seg.at[plane, xx], here
+    ).wait_recv()
+    seg_wait(1, other)
+    own_piece.wait()
+    for pair in pairs[1:]:
+        kv_wait(1, *pair)
+
+    @pl.when(z > 0)
+    def _():
+        for xx in range(nx):
+            seg_wait(0, xx)
+        for pair in pairs:
+            kv_wait(0, *pair)
+
+    key_seg = jnp.concatenate(
+        [seg_buf[plane, xx] for plane in range(2) for xx in range(nx)], axis=1
+    )
+    own_seg_row = key_seg[:, rows:]
+    seg_column = jnp.transpose(jnp.broadcast_to(own_seg_row, (HD, rows)))[:, :1]
+    key_pos = lax.broadcasted_iota(jnp.int32, (1, 2 * rows), 1) - rows
+    keys = [
+        jnp.concatenate([kv_all[0, xx], kv_all[1, xx]], axis=0) for xx in range(nx)
+    ]
+    step_rows = rows // nf
+    for b in range(nf):
+        span = slice(b * step_rows, (b + 1) * step_rows)
+        query_pos = b * step_rows + lax.broadcasted_iota(jnp.int32, (step_rows, 1), 0)
+        score = None
+        for xx in range(nx):
+            term = lax.dot_general(
+                quarters[xx][span], keys[xx], (((1,), (1,)), ((), ())),
+                preferred_element_type=f32,
+            )
+            score = term if score is None else score + term
+        allowed = (key_pos <= query_pos) & (key_seg == seg_column[span])
+        masked = jnp.where(allowed, score * HD ** (-0.5), NEG_FILL)
+        row_max = jnp.max(masked, axis=1, keepdims=True)
+        weight = jnp.where(allowed, jnp.exp(masked - row_max), 0.0)
+        row_total = jnp.sum(weight, axis=1, keepdims=True)
+        rounded = weight.astype(bf16)
+        product = [
+            jnp.dot(rounded, keys[xx], preferred_element_type=f32) for xx in range(nx)
+        ]
+        mixed = None
+        for xx in reversed(range(nx)):
+            low = pltpu.roll(product[xx], (half + xx * quarter) % HD, 1)
+            high = pltpu.roll(product[xx], (HD - (nx - 1 - xx) * quarter) % HD, 1)
+            lane_block = lane // quarter
+            value = jnp.where(lane_block < nx, low, high)
+            mixed = value if mixed is None else jnp.where(lane_block % nx == xx, value, mixed)
+        mix_own[span, :] = (mixed / row_total).astype(bf16)
+
+    wo_end(1)
+    head = f * nx + x
+
+    def mix_send(dx, d):
+        ff, xx = lax.rem(f + d, nf), lax.rem(x + dx, nx)
+        return remote(
+            mix_own.at[tile(xx, tok)], mix_buf.at[:, tile(head, HD)],
+            s_mix.at[dx, d], r_mix.at[x, f], dev(ff, z, xx),
+        )
+
+    def mix_wait(dx, d):
+        ff, xx = lax.rem(f + d, nf), lax.rem(x + dx, nx)
+        remote(
+            mix_own.at[tile(x, tok)], mix_buf.at[:, tile(ff * nx + xx, HD)],
+            s_mix.at[dx, d], r_mix.at[xx, ff], here,
+        ).wait_recv()
+
+    for pair in pairs[1:]:
+        mix_send(*pair).start()
+    own_mix = pltpu.make_async_copy(
+        mix_own.at[tile(x, tok)], mix_buf.at[:, tile(head, HD)], s_loc.at[6]
+    )
+    own_mix.start()
+    for d in range(2, nz):
+        wo_end(d)
+    own_mix.wait()
+    own_wo.wait()
+    for pair in pairs[1:]:
+        mix_wait(*pair)
+    for c in range(WO_CHUNKS):
+        for j in range(nz):
+            wo_wait(j, other, c)
+        out[:, c * chunk : (c + 1) * chunk] = jnp.dot(
+            mix_buf[...], wo_buf[:, c * chunk : (c + 1) * chunk], preferred_element_type=f32
+        ).astype(bf16)
+
+    hid_send.wait_send()
+    seg_same.wait_send()
+    for d in range(1, nz):
+        wkv_send(d).wait_send()
+    for d in range(1, nf):
+        kvp_send(d).wait_send()
+        q_send(lax.rem(f + d, nf)).wait_send()
+    for pair in pairs[1:]:
+        kv_send(1, *pair).wait_send()
+        mix_send(*pair).wait_send()
+
+    @pl.when(z < nz - 1)
+    def _():
+        for xx in range(nx):
+            seg_next(xx).wait_send()
+        for pair in pairs:
+            kv_send(0, *pair).wait_send()
+
+    for j in range(nz):
+        for c in range(WO_CHUNKS):
+            wo_cross(j, c).wait_send()
+
+        @pl.when((z < nz - 1) & (z >= j))
+        def _():
+            wq_copy(wq, j, True).wait_send()
+            for c in range(WO_CHUNKS):
+                wo_copy(j, c, True).wait_send()
+
+        @pl.when((z > 0) & (z <= j))
+        def _():
+            wq_copy(wq, j, False).wait_send()
+            for c in range(WO_CHUNKS):
+                wo_copy(j, c, False).wait_send()
+
+
+def fused_on_device(nf, nz, nx, hidden, w_query, w_keyvalue, w_output, segment_ids):
+    tok, kdim = hidden.shape
+    cols = w_output.shape[1]
+    rows = tok * nx
+    sub = rows // nf
+    kvw = w_keyvalue.shape[1]
+    f32, bf16 = jnp.float32, jnp.bfloat16
+    dma = pltpu.SemaphoreType.DMA
+    vmem = pl.BlockSpec(memory_space=pltpu.VMEM)
+    scratch = [
+        pltpu.VMEM((rows, kdim), bf16),
+        pltpu.VMEM((nz, kdim, HD), bf16),
+        pltpu.VMEM((nz * kvw, kdim), bf16),
+        pltpu.VMEM((nz * nx * HD, cols), bf16),
+        pltpu.VMEM((2, nx, 1, tok), jnp.int32),
+        pltpu.VMEM((nz, rows, HD), f32),
+        pltpu.VMEM((nf, rows, HD), f32),
+        pltpu.VMEM((rows, nz * kvw), f32),
+        pltpu.VMEM((nf, sub, nz * kvw), f32),
+        pltpu.VMEM((sub, HD), bf16),
+        pltpu.VMEM((2, nx, rows, HD), bf16),
+        pltpu.VMEM((rows, HD), bf16),
+        pltpu.VMEM((tok, nz * nx * HD), bf16),
+        dma((7,)), dma, dma, dma((1 + nx,)), dma((2, nx)),
+        dma((nz,)), dma((nz,)), dma((nz,)), dma((nz,)), dma((nz,)),
+        dma((nz,)), dma((nf,)), dma((nf,)), dma((nf,)),
+        dma((2, nx, nf)), dma((2, nx, nf)),
+        dma((nz, WO_CHUNKS)), dma((nz, WO_CHUNKS)), dma((nz, WO_CHUNKS)),
+        dma((nz * nx, WO_CHUNKS)), dma((nx, nf)), dma((nx, nf)),
+    ]
+    return pl.pallas_call(
+        functools.partial(fused_kernel, nf, nz, nx),
+        out_shape=jax.ShapeDtypeStruct((tok, cols), bf16),
+        in_specs=[vmem] * 5,
+        out_specs=vmem,
+        scratch_shapes=scratch,
+        name="fused_sublayer",
+        compiler_params=pltpu.CompilerParams(
+            has_side_effects=True, vmem_limit_bytes=60 * 1024 * 1024
+        ),
+    )(hidden, w_query, w_keyvalue.T, w_output, segment_ids.reshape(1, tok))
+
+
 def solution(mesh):
     in_specs = (P("sp", "fsdp"), P("fsdp", "sp"), P("fsdp", "sp"), P("sp", "fsdp"), P("sp"))
     out_specs = P("sp", "fsdp")
+    nf, sp = mesh.shape["fsdp"], mesh.shape["sp"]
+    if sp == GROUP and sp == 2 * nf:
+        body = functools.partial(fused_on_device, nf, nf, sp // nf)
+    else:
+        body = on_device
     return jax.shard_map(
-        on_device, mesh=mesh, in_specs=in_specs, out_specs=out_specs, check_vma=False
-    )
+        body, mesh=mesh, in_specs=in_specs, out_specs=out_specs, check_vma=False
+    )

time: 281 us -> 114 us (0.41); the launches traced: 277 us -> 114 us
  waiting for transfers between devices: 175 us -> 0 us
  Pallas kernels: 0 us -> 112 us
  blocking collectives: 47.5 us -> 0 us
  matrix products: 14.9 us -> 0 us
  local copies, waits for them, and re-layouts: 17 us -> 2.3 us
  between operations: 13.7 us -> 0.01 us
  starting transfers between devices: 6.22 us -> 0 us
  other arithmetic: 3.13 us -> 0 us
    all_gather x4 -> x0, waiting for transfers between devices: 142 us -> none  [the longest x1 72.3 us: on_device(): query_part = project(lax.all_gather(w_query, 'sp', axis=1, tiled=True))]
    pallas_call x0 -> x1, Pallas kernels: none -> 112 us  [fused_on_device(): pl.pallas_call(functools.partial(fused_kernel, nf, nz, nx), out_shape=jax...]
    reduce_scatter x2 -> x0, waiting for transfers between devices: 31.3 us -> none  [the longest x1 18.1 us: on_device(): lax.psum_scatter(kv_part, 'fsdp', scatter_dimension=0, tiled=True)]
    all_to_all x2 -> x0, blocking collectives: 25.1 us -> none  [the longest x1 13.2 us: on_device(): lax.all_to_all(attention, 'sp', split_axis=0, concat_axis=1, tiled=True)]
    all_gather x2 -> x0, blocking collectives: 22.4 us -> none  [the longest x1 15.9 us: on_device(): segment_all = lax.all_gather(segment_ids, 'sp', axis=0, tiled=True)]
    gather x2 -> x0, local copies, waits for them, and re-layouts: 14.9 us -> none  [the longest x1 11.8 us: on_device(): key_seg = segment_all[key_pos]]
    dot_general x5 -> x0, matrix products: 14.9 us -> none  [the longest x2 6.83 us: project(): return jnp.dot(hidden, weight_block, preferred_element_type=jnp.float32)]
    all_to_all x1 -> x0, starting transfers between devices: 6.02 us -> none  [on_device(): lax.all_to_all(query_local, 'sp', split_axis=1, concat_axis=0, tiled=True)]
  transfers between devices with their start and end apart: 7 -> 0, of which waited for: 5 -> 0; matrix products, arithmetic and copies ran while one was open for 11% -> 0% of each run, Pallas kernels for 0% -> 0%
where the time goes in v1:
time: 114 us
  Pallas kernels  112 us (98%)
  local copies, waits for them, and re-layouts  2.3 us (2%)
    pallas_call x1, Pallas kernels, fused_on_device(): pl.pallas_call(functools.partial(fused_kernel, nf, nz, nx), out_shape=jax...  112 us
    unnamed x1, local copies, waits for them, and re-layouts  2.3 us

profile of v1, /device:TPU:24, one launch (start us, length us, event | category | flops | bytes accessed | tf_op | source)
XLA Modules:
  0.0 114.1 jit_solution(12716811806171409058)
XLA Ops:
  0.0 111.8 %fused_sublayer.1 = bf16[256,2048]{1,0:T(8,128)(2,1)} custom-call(bf16[256,2048]{1,0:T(8,128)(2,1)} %hid.1, bf16[2048,128]{1,0:T(8,128)(2,1)} %wq.1, bf16[32,2048]{1,0:T(8,128)(2,1)} %bitcast.2, bf16[128,2048]{1,0:T(8,128)(2,1)} %wo.1, s32[1,256]{1,0:T(1,128)} %bitcast.3), custom_call_target="tpu_custom_call" | custom-call | tf_op jit(solution)/shard_map/fused_sublayer/pallas_call | solution.py:592
  111.8 2.3 %copy.7 = bf16[256,2048]{1,0:T(8,128)(2,1)} copy(bf16[256,2048]{1,0:T(8,128)(2,1)} %fused_sublayer.1) | data formatting | bytes 2097152

commit v2 on v1

--- a/solution.py
+++ b/solution.py
@@ -130,7 +130,7 @@
 
 
 NEG_POS = -1
-WO_CHUNKS = 2
+WO_CHUNKS = 4
 
 
 def fused_kernel(
@@ -228,6 +228,31 @@
             seg, seg_buf.at[0, x], s_seg.at[1 + xx], r_seg.at[0, x], dev(f, z + 1, xx)
         )
 
+    barrier = pltpu.get_barrier_semaphore()
+
+    def greet(ff, zz, xx):
+        pl.semaphore_signal(
+            barrier, inc=1, device_id=dev(ff, zz, xx), device_id_type=pl.DeviceIdType.MESH
+        )
+
+    plane = nf * nx
+    for step in (1, -1):
+        @pl.when((z + step >= 0) & (z + step < nz))
+        def _():
+            for xx in range(nx):
+                for ff in range(nf):
+                    greet(ff, z + step, xx)
+
+        for far in range(2, nz):
+            @pl.when((z + far * step >= 0) & (z + far * step < nz))
+            def _():
+                greet(f, z + far * step, x)
+
+    for d in range(1, plane):
+        greet(lax.rem(f + d, nf), z, lax.rem(x + d // nf, nx))
+    ends = jnp.where(z == 0, 1, 0) + jnp.where(z == nz - 1, 1, 0)
+    pl.semaphore_wait(barrier, (3 - ends) * plane - 1 + nz - 3 + ends)
+
     for d in range(1, nz):
         wkv_send(d).start()
 
@@ -347,6 +372,8 @@
 
     for d in range(1, nf):
         kvp_send(d).start()
+    if nz > 2:
+        wq_step(2)
     q_project(z)
     q_step(1)
     total = kv_part[tile(f, sub), :]
@@ -385,7 +412,8 @@
             kv_send(0, *pair).start()
 
     for d in range(2, nz):
-        wq_step(d)
+        if d > 2:
+            wq_step(d)
         q_step(d)
 
     def wo_side(j, to_right):
@@ -488,7 +516,6 @@
             mixed = value if mixed is None else jnp.where(lane_block % nx == xx, value, mixed)
         mix_own[span, :] = (mixed / row_total).astype(bf16)
 
-    wo_end(1)
     head = f * nx + x
 
     def mix_send(dx, d):
@@ -511,13 +538,24 @@
         mix_own.at[tile(x, tok)], mix_buf.at[:, tile(head, HD)], s_loc.at[6]
     )
     own_mix.start()
-    for d in range(2, nz):
+    for d in range(1, nz - 1):
         wo_end(d)
     own_mix.wait()
     own_wo.wait()
     for pair in pairs[1:]:
         mix_wait(*pair)
+
+    def wo_last(c):
+        for end, j in ((0, nz - 1), (nz - 1, 0)):
+            @pl.when(z == end)
+            def _():
+                wo_wait(j, x, c)
+                wo_cross(j, c).start()
+
+    wo_last(0)
     for c in range(WO_CHUNKS):
+        if c + 1 < WO_CHUNKS:
+            wo_last(c + 1)
         for j in range(nz):
             wo_wait(j, other, c)
         out[:, c * chunk : (c + 1) * chunk] = jnp.dot(
@@ -597,7 +635,7 @@
         scratch_shapes=scratch,
         name="fused_sublayer",
         compiler_params=pltpu.CompilerParams(
-            has_side_effects=True, vmem_limit_bytes=60 * 1024 * 1024
+            collective_id=0, has_side_effects=True, vmem_limit_bytes=60 * 1024 * 1024
         ),
     )(hidden, w_query, w_keyvalue.T, w_output, segment_ids.reshape(1, tok))
 

time: 114 us -> 121 us (1.061)
  Pallas kernels: 112 us -> 118 us
    pallas_call x1, Pallas kernels: 112 us -> 118 us  [fused_on_device(): pl.pallas_call(functools.partial(fused_kernel, nf, nz, nx), out_shape=jax...]
where the time goes in v2:
time: 121 us; the launch traced here: 120 us
  Pallas kernels  118 us (98%)
  local copies, waits for them, and re-layouts  2.3 us (2%)
    pallas_call x1, Pallas kernels, fused_on_device(): pl.pallas_call(functools.partial(fused_kernel, nf, nz, nx), out_shape=jax...  118 us

profile of v2, /device:TPU:24, one launch (start us, length us, event | category | flops | bytes accessed | tf_op | source)
XLA Modules:
  0.0 120.4 jit_solution(16649692479110707122)
XLA Ops:
  0.0 118.1 %fused_sublayer.1 = bf16[256,2048]{1,0:T(8,128)(2,1)} custom-call(bf16[256,2048]{1,0:T(8,128)(2,1)} %hid.1, bf16[2048,128]{1,0:T(8,128)(2,1)} %wq.1, bf16[32,2048]{1,0:T(8,128)(2,1)} %bitcast.2, bf16[128,2048]{1,0:T(8,128)(2,1)} %wo.1, s32[1,256]{1,0:T(1,128)} %bitcast.3), custom_call_target="tpu_custom_call" | custom-call | tf_op jit(solution)/shard_map/fused_sublayer/pallas_call | solution.py:630
  118.1 2.3 %copy.7 = bf16[256,2048]{1,0:T(8,128)(2,1)} copy(bf16[256,2048]{1,0:T(8,128)(2,1)} %fused_sublayer.1) | data formatting | bytes 2097152

commit v3 on v2

--- a/solution.py
+++ b/solution.py
@@ -136,7 +136,7 @@
 def fused_kernel(
     nf, nz, nx, hid, wq, wkv, wo, seg, out,
     h_buf, wq_buf, wkv_buf, wo_buf, seg_buf,
-    q_part, q_recv, kv_part, kv_recv, kv_piece, kv_all, mix_own, mix_buf,
+    q_part, q_recv, kv_part, kv_recv, kv_piece, kv_all, mix_own, mix_buf, q_cos, q_sin,
     s_loc, s_hid, r_hid, s_seg, r_seg, s_wkv, r_wkv, s_wqr, s_wql, r_wq,
     s_q, r_q, s_kvp, r_kvp, s_kv, r_kv, s_wor, s_wol, s_wox, r_wo, s_mix, r_mix,
 ):
@@ -298,6 +298,10 @@
     kv_cos = jnp.where(is_key, jnp.cos(kv_angle), 1.0)
     kv_sin = jnp.where(is_key, jnp.sin(kv_angle), 0.0)
     kv_sin = jnp.where(lane < quarter, -kv_sin, kv_sin)
+    q_angle = table(rows, z * rows, lane % half)
+    q_sine = jnp.sin(q_angle)
+    q_cos[...] = jnp.cos(q_angle)
+    q_sin[...] = jnp.where(lane < half, -q_sine, q_sine)
 
     def wq_step(d):
         @pl.when(z >= d)
@@ -390,9 +394,16 @@
 
     def kv_send(plane, dx, d):
         ff, xx = lax.rem(f + d, nf), lax.rem(x + dx, nx)
-        return remote(
-            kv_piece, kv_all.at[plane, x, piece_rows],
-            s_kv.at[plane, dx, d], r_kv.at[plane, x, f], dev(ff, z + 1 - plane, xx),
+        slot = kv_all.at[plane, x, piece_rows]
+        return remote(
+            kv_piece if plane else slot, slot,
+            s_kv.at[plane, dx, d], r_kv.at[plane, x, f], dev(ff, z, xx),
+        )
+
+    def kv_next():
+        return remote(
+            kv_piece, kv_all.at[0, x, piece_rows],
+            s_kv.at[0, 0, 0], r_kv.at[0, x, f], dev(f, z + 1, x),
         )
 
     def kv_wait(plane, dx, d):
@@ -408,19 +419,24 @@
 
     @pl.when(z < nz - 1)
     def _():
-        for pair in pairs:
+        kv_next().start()
+
+    q_step(2)
+
+    @pl.when(z > 0)
+    def _():
+        kv_wait(0, 0, 0)
+        for pair in pairs[1:]:
             kv_send(0, *pair).start()
 
-    for d in range(2, nz):
-        if d > 2:
-            wq_step(d)
+    for d in range(3, nz):
+        wq_step(d)
         q_step(d)
 
     def wo_side(j, to_right):
         for c in range(WO_CHUNKS):
             wo_wait(j, x, c)
-            if to_right is not None:
-                wo_copy(j, c, to_right).start()
+            wo_copy(j, c, to_right).start()
             wo_cross(j, c).start()
 
     def wo_mid(d):
@@ -432,28 +448,22 @@
         def _():
             wo_side(z + d, False)
 
-    def wo_end(d):
-        if d < nz:
-            @pl.when((z >= d) & (z == nz - 1))
+    def wo_end(d, c):
+        for end, j in ((0, d), (nz - 1, nz - 1 - d)):
+            @pl.when(z == end)
             def _():
-                wo_side(z - d, None)
-
-            @pl.when((z + d < nz) & (z == 0))
-            def _():
-                wo_side(z + d, None)
+                wo_wait(j, x, c)
+                wo_cross(j, c).start()
 
     for d in range(1, nz - 1):
         wo_mid(d)
 
-    q_angle = table(rows, z * rows, lane % half)
-    q_cos = jnp.cos(q_angle)
-    q_sin = jnp.where(lane < half, -jnp.sin(q_angle), jnp.sin(q_angle))
     q_total = q_part[f]
     for d in range(1, nf):
         ff = lax.rem(f + d, nf)
         remote(q_part.at[0], q_recv.at[ff], s_q.at[0], r_q.at[ff], here).wait_recv()
         q_total = q_total + q_recv[ff]
-    q_turned = q_total * q_cos + pltpu.roll(q_total, half, 1) * q_sin
+    q_turned = q_total * q_cos[...] + pltpu.roll(q_total, half, 1) * q_sin[...]
     q_head = q_turned.astype(bf16).astype(f32)
     quarters = []
     for xx in range(nx):
@@ -475,7 +485,7 @@
     def _():
         for xx in range(nx):
             seg_wait(0, xx)
-        for pair in pairs:
+        for pair in pairs[1:]:
             kv_wait(0, *pair)
 
     key_seg = jnp.concatenate(
@@ -515,6 +525,8 @@
             value = jnp.where(lane_block < nx, low, high)
             mixed = value if mixed is None else jnp.where(lane_block % nx == xx, value, mixed)
         mix_own[span, :] = (mixed / row_total).astype(bf16)
+        for c in range(b * WO_CHUNKS // nf, (b + 1) * WO_CHUNKS // nf):
+            wo_end(1, c)
 
     head = f * nx + x
 
@@ -538,24 +550,17 @@
         mix_own.at[tile(x, tok)], mix_buf.at[:, tile(head, HD)], s_loc.at[6]
     )
     own_mix.start()
-    for d in range(1, nz - 1):
-        wo_end(d)
+    for d in range(2, nz - 1):
+        for c in range(WO_CHUNKS):
+            wo_end(d, c)
     own_mix.wait()
     own_wo.wait()
     for pair in pairs[1:]:
         mix_wait(*pair)
-
-    def wo_last(c):
-        for end, j in ((0, nz - 1), (nz - 1, 0)):
-            @pl.when(z == end)
-            def _():
-                wo_wait(j, x, c)
-                wo_cross(j, c).start()
-
-    wo_last(0)
+    wo_end(nz - 1, 0)
     for c in range(WO_CHUNKS):
         if c + 1 < WO_CHUNKS:
-            wo_last(c + 1)
+            wo_end(nz - 1, c + 1)
         for j in range(nz):
             wo_wait(j, other, c)
         out[:, c * chunk : (c + 1) * chunk] = jnp.dot(
@@ -577,7 +582,11 @@
     def _():
         for xx in range(nx):
             seg_next(xx).wait_send()
-        for pair in pairs:
+        kv_next().wait_send()
+
+    @pl.when(z > 0)
+    def _():
+        for pair in pairs[1:]:
             kv_send(0, *pair).wait_send()
 
     for j in range(nz):
@@ -620,6 +629,8 @@
         pltpu.VMEM((2, nx, rows, HD), bf16),
         pltpu.VMEM((rows, HD), bf16),
         pltpu.VMEM((tok, nz * nx * HD), bf16),
+        pltpu.VMEM((rows, HD), f32),
+        pltpu.VMEM((rows, HD), f32),
         dma((7,)), dma, dma, dma((1 + nx,)), dma((2, nx)),
         dma((nz,)), dma((nz,)), dma((nz,)), dma((nz,)), dma((nz,)),
         dma((nz,)), dma((nf,)), dma((nf,)), dma((nf,)),

time: 121 us -> 120 us (level)
  no operation moved by 1% of the time
where the time goes in v3:
time: 120 us
  Pallas kernels  117 us (98%)
  local copies, waits for them, and re-layouts  2.3 us (2%)
    pallas_call x1, Pallas kernels, fused_on_device(): pl.pallas_call(functools.partial(fused_kernel, nf, nz, nx), out_shape=jax...  117 us

profile of v3, /device:TPU:24, one launch (start us, length us, event | category | flops | bytes accessed | tf_op | source)
XLA Modules:
  0.0 119.6 jit_solution(14540279795446109858)
XLA Ops:
  0.0 117.3 %fused_sublayer.1 = bf16[256,2048]{1,0:T(8,128)(2,1)} custom-call(bf16[256,2048]{1,0:T(8,128)(2,1)} %hid.1, bf16[2048,128]{1,0:T(8,128)(2,1)} %wq.1, bf16[32,2048]{1,0:T(8,128)(2,1)} %bitcast.2, bf16[128,2048]{1,0:T(8,128)(2,1)} %wo.1, s32[1,256]{1,0:T(1,128)} %bitcast.3), custom_call_target="tpu_custom_call" | custom-call | tf_op jit(solution)/shard_map/fused_sublayer/pallas_call | solution.py:641
  117.3 2.3 %copy.7 = bf16[256,2048]{1,0:T(8,128)(2,1)} copy(bf16[256,2048]{1,0:T(8,128)(2,1)} %fused_sublayer.1) | data formatting | bytes 2097152

commit v4 on v3

--- a/solution.py
+++ b/solution.py
@@ -264,6 +264,14 @@
     def _():
         wq_copy(wq, z, False).start()
 
+    @pl.when(z == nz - 2)
+    def _():
+        wo_own(True)
+
+    @pl.when(z == 1)
+    def _():
+        wo_own(False)
+
     hid_send.start()
     seg_same.start()
 
@@ -313,7 +321,7 @@
             def _():
                 wq_copy(wq_buf.at[j], j, True).start()
 
-                @pl.when(z == d)
+                @pl.when((z == d) & (z != nz - 2))
                 def _():
                     wo_own(True)
 
@@ -326,7 +334,7 @@
             def _():
                 wq_copy(wq_buf.at[j], j, False).start()
 
-                @pl.when(z + d == nz - 1)
+                @pl.when((z + d == nz - 1) & (z != 1))
                 def _():
                     wo_own(False)
 
@@ -348,6 +356,13 @@
         @pl.when(z + d < nz)
         def _():
             q_project(z + d)
+
+    def wo_end(d, c):
+        for end, j in ((0, d), (nz - 1, nz - 1 - d)):
+            @pl.when(z == end)
+            def _():
+                wo_wait(j, x, c)
+                wo_cross(j, c).start()
 
     wq_step(1)
     own_h.wait()
@@ -376,8 +391,12 @@
 
     for d in range(1, nf):
         kvp_send(d).start()
-    if nz > 2:
+    inner = (z > 0) & (z < nz - 1)
+
+    @pl.when(inner)
+    def _():
         wq_step(2)
+
     q_project(z)
     q_step(1)
     total = kv_part[tile(f, sub), :]
@@ -421,6 +440,13 @@
     def _():
         kv_next().start()
 
+    for c in range(WO_CHUNKS):
+        wo_end(1, c)
+
+    @pl.when(jnp.logical_not(inner))
+    def _():
+        wq_step(2)
+
     q_step(2)
 
     @pl.when(z > 0)
@@ -447,13 +473,6 @@
         @pl.when((z + d < nz) & (z > 0))
         def _():
             wo_side(z + d, False)
-
-    def wo_end(d, c):
-        for end, j in ((0, d), (nz - 1, nz - 1 - d)):
-            @pl.when(z == end)
-            def _():
-                wo_wait(j, x, c)
-                wo_cross(j, c).start()
 
     for d in range(1, nz - 1):
         wo_mid(d)
@@ -525,8 +544,6 @@
             value = jnp.where(lane_block < nx, low, high)
             mixed = value if mixed is None else jnp.where(lane_block % nx == xx, value, mixed)
         mix_own[span, :] = (mixed / row_total).astype(bf16)
-        for c in range(b * WO_CHUNKS // nf, (b + 1) * WO_CHUNKS // nf):
-            wo_end(1, c)
 
     head = f * nx + x
 

time: 120 us -> 105 us (0.88)
  Pallas kernels: 117 us -> 103 us
    pallas_call x1, Pallas kernels: 117 us -> 103 us  [fused_on_device(): pl.pallas_call(functools.partial(fused_kernel, nf, nz, nx), out_shape=jax...]
where the time goes in v4:
time: 105 us
  Pallas kernels  103 us (98%)
  local copies, waits for them, and re-layouts  2.3 us (2%)
    pallas_call x1, Pallas kernels, fused_on_device(): pl.pallas_call(functools.partial(fused_kernel, nf, nz, nx), out_shape=jax...  103 us
    unnamed x1, local copies, waits for them, and re-layouts  2.3 us

profile of v4, /device:TPU:24, one launch (start us, length us, event | category | flops | bytes accessed | tf_op | source)
XLA Modules:
  0.0 104.9 jit_solution(8740777669122016673)
XLA Ops:
  0.0 102.6 %fused_sublayer.1 = bf16[256,2048]{1,0:T(8,128)(2,1)} custom-call(bf16[256,2048]{1,0:T(8,128)(2,1)} %hid.1, bf16[2048,128]{1,0:T(8,128)(2,1)} %wq.1, bf16[32,2048]{1,0:T(8,128)(2,1)} %bitcast.2, bf16[128,2048]{1,0:T(8,128)(2,1)} %wo.1, s32[1,256]{1,0:T(1,128)} %bitcast.3), custom_call_target="tpu_custom_call" | custom-call | tf_op jit(solution)/shard_map/fused_sublayer/pallas_call | solution.py:658
  102.6 2.3 %copy.7 = bf16[256,2048]{1,0:T(8,128)(2,1)} copy(bf16[256,2048]{1,0:T(8,128)(2,1)} %fused_sublayer.1) | data formatting | bytes 2097152

commit v5 on v4

--- a/solution.py
+++ b/solution.py
@@ -544,6 +544,9 @@
             value = jnp.where(lane_block < nx, low, high)
             mixed = value if mixed is None else jnp.where(lane_block % nx == xx, value, mixed)
         mix_own[span, :] = (mixed / row_total).astype(bf16)
+        if nz > 3:
+            for c in range(b * WO_CHUNKS // nf, (b + 1) * WO_CHUNKS // nf):
+                wo_end(2, c)
 
     head = f * nx + x
 
@@ -567,7 +570,7 @@
         mix_own.at[tile(x, tok)], mix_buf.at[:, tile(head, HD)], s_loc.at[6]
     )
     own_mix.start()
-    for d in range(2, nz - 1):
+    for d in range(3 if nz > 3 else 2, nz - 1):
         for c in range(WO_CHUNKS):
             wo_end(d, c)
     own_mix.wait()

time: 105 us -> 106 us (level)
  the two profiles are of different devices: /device:TPU:24 before, /device:TPU:0 now
where the time goes in v5:
time: 106 us; the launch traced here: 105 us
  Pallas kernels  103 us (97%)
  local copies, waits for them, and re-layouts  2.3 us (2%)
    pallas_call x1, Pallas kernels, fused_on_device(): pl.pallas_call(functools.partial(fused_kernel, nf, nz, nx), out_shape=jax...  103 us
    unnamed x1, local copies, waits for them, and re-layouts  2.3 us

profile of v5, /device:TPU:0, one launch (start us, length us, event | category | flops | bytes accessed | tf_op | source)
XLA Modules:
  0.0 105.4 jit_solution(7271911433237234698)
XLA Ops:
  0.0 103.1 %fused_sublayer.1 = bf16[256,2048]{1,0:T(8,128)(2,1)} custom-call(bf16[256,2048]{1,0:T(8,128)(2,1)} %hid.1, bf16[2048,128]{1,0:T(8,128)(2,1)} %wq.1, bf16[32,2048]{1,0:T(8,128)(2,1)} %bitcast.2, bf16[128,2048]{1,0:T(8,128)(2,1)} %wo.1, s32[1,256]{1,0:T(1,128)} %bitcast.3), custom_call_target="tpu_custom_call" | custom-call | tf_op jit(solution)/shard_map/fused_sublayer/pallas_call | solution.py:661
  103.1 2.3 %copy.7 = bf16[256,2048]{1,0:T(8,128)(2,1)} copy(bf16[256,2048]{1,0:T(8,128)(2,1)} %fused_sublayer.1) | data formatting | bytes 2097152
